TPU v7x, 128 devices: a whole 4x4x4 slice. The times are simulated.
128 devices in a mesh: row: 8 (over z, core), col: 16 (over y, x).
Axes of the slice: x: 4, y: 4, z: 4, core: 2. Of those that a mesh axis runs over, the one named last changes fastest.
Arguments:
- ainv_anc: bfloat16 [24576, 24576], P('row', 'col'), may hold values from -6 to 6
- l_panel: bfloat16 [1536, 24576], P('col', 'row'), may hold values from -0.078125 to 0.078125
- diag_inv: float32 [1536, 768], P('col', 'row'), may hold values from -6 to 6
- struct_mask: int32 [2, 192], replicated, may hold values 0 or 1
- pieces: float32 [24576, 32, 128], P(('row', 'col')), may hold values from -6 to 6
- tile_owner: int32 [24576, 1], P(('row', 'col')), may hold values from 0 to 127; in each aligned block of 192 rows (0 to 191, 192 to 383, ...) at most 3 rows name the same one
Outputs:
- ainv_upper: bfloat16 [1536, 24576], P('col', 'row')
- ainv_diag: float32 [1536, 768], P('col', 'row')
- moved: float32 [49152, 32, 128], P(('row', 'col'))
Inputs may be any that keep to these rules, and one draw needn't show every extreme that they name: `tile_owner`: among the 192 pieces of one device no owner is named more than 3 times, a bound that some block reaches.
All inputs are finite; a program needn't handle non-finite values.
Results may differ from a plain program's by a relative error of at most 0.015.
Values may be sent and summed in bfloat16 or wider, within the bound.
A program may use at most 128 MiB of HBM per device.

v0:
```python
import jax
import jax.numpy as jnp
from jax import lax
from jax.sharding import PartitionSpec as P

W = 768
AB = 128
SLOT = 3


def broadcast(value, axis, root):
    mine = lax.axis_index(axis) == root
    return lax.psum(jnp.where(mine, value, jnp.zeros_like(value)), axis)


def cut_along(value, dim, count):
    before, after = (value.shape[:dim], value.shape[dim + 1 :])
    return jnp.moveaxis(value.reshape(*before, count, -1, *after), dim, 0)


def sum_at_owner(value, axis, dim):
    parts = cut_along(value, dim, lax.axis_size(axis))
    arrived = lax.all_to_all(parts, axis, split_axis=0, concat_axis=0, tiled=True)
    return arrived.astype(jnp.float32).sum(axis=0)


def joined_along(parts, dim):
    shape = list(parts.shape[1:])
    shape[dim] *= parts.shape[0]
    return jnp.moveaxis(parts, 0, dim).reshape(shape)


def joined_exchange(value, axis, axes, splits, concats):
    sizes = [lax.axis_size(a) for a in axes]
    parts = cut_along(value, splits[0], sizes[0])
    parts = jnp.moveaxis(cut_along(parts, splits[1] + 1, sizes[1]), 0, 1)
    inside = parts.shape[2:]
    parts = parts.reshape(-1, *inside)
    parts = lax.all_to_all(parts, axis, split_axis=0, concat_axis=0, tiled=True)
    parts = joined_along(parts.reshape(*sizes, *inside), concats[0] + 1)
    return joined_along(parts, concats[1])


def local(ainv_anc, l_panel, diag_inv, struct_mask, pieces, tile_owner):
    row_devices = lax.axis_size("row")
    col_devices = lax.axis_size("col")
    row_index = lax.axis_index("row")
    col_index = lax.axis_index("col")
    slab_rows = l_panel.shape[0]
    local_rows = l_panel.shape[1]
    cross_width = ainv_anc.shape[1]
    group_ratio = col_devices // row_devices
    supernode = col_index * slab_rows // W
    block_count = local_rows // AB
    keep_blocks = lax.dynamic_slice(
        struct_mask, (supernode, row_index * block_count), (1, block_count)
    )
    keep_rows = (
        jnp.broadcast_to(keep_blocks[:, :, None], (1, block_count, AB)).reshape(1, local_rows) > 0
    )
    masked = jnp.where(keep_rows, l_panel, jnp.zeros_like(l_panel))
    gathered = lax.all_gather(masked, "col", axis=0, tiled=True)
    offset = col_index % group_ratio * cross_width
    own_cross = lax.dynamic_slice_in_dim(gathered, offset, cross_width, 1)
    cross_rows = broadcast(own_cross, "row", col_index // group_ratio)
    product = lax.psum_scatter(
        lax.dot_general(
            cross_rows, ainv_anc, (((1,), (1,)), ((), ())), preferred_element_type=jnp.float32
        ).astype(jnp.bfloat16),
        "col",
        scatter_dimension=0,
        tiled=True,
    ).astype(jnp.float32)
    upper_rows = jnp.where(keep_rows, -product, jnp.zeros_like(product)).astype(jnp.bfloat16)
    own_block = lax.dynamic_slice_in_dim(gathered, supernode * W, W, 0)
    diag_part = lax.dot_general(
        upper_rows, own_block, (((1,), (1,)), ((), ())), preferred_element_type=jnp.float32
    )
    summed = sum_at_owner(diag_part.astype(jnp.bfloat16), "row", 1)
    ainv_diag = diag_inv - summed
    devices_all = row_devices * col_devices
    owners = tile_owner[:, 0]
    onehot = (owners[:, None] == jnp.arange(devices_all, dtype=jnp.int32)[None, :]).astype(
        jnp.int32
    )
    earlier = jnp.cumsum(onehot, axis=0) - onehot
    rank_in_dest = jnp.sum(earlier * onehot, axis=1)
    slot_index = owners * SLOT + rank_in_dest
    piece_rows = pieces.shape[1]
    piece_cols = pieces.shape[2]
    buffer = (
        jnp.zeros((devices_all * SLOT, piece_rows, piece_cols), jnp.float32)
        .at[slot_index]
        .set(pieces)
    )
    shaped = buffer.reshape(row_devices, col_devices, SLOT, piece_rows, piece_cols)
    arrived = joined_exchange(
        shaped.astype(jnp.bfloat16), ("row", "col"), ("row", "col"), (0, 1), (0, 1)
    ).astype(shaped.dtype)
    moved_pieces = arrived.reshape(devices_all * SLOT, piece_rows, piece_cols)
    return (upper_rows, ainv_diag, moved_pieces)


def solution(mesh):
    in_specs = (
        P("row", "col"),
        P("col", "row"),
        P("col", "row"),
        P(),
        P(("row", "col"), None, None),
        P(("row", "col"), None),
    )
    out_specs = (P("col", "row"), P("col", "row"), P(("row", "col"), None, None))
    return jax.shard_map(local, mesh=mesh, in_specs=in_specs, out_specs=out_specs, check_vma=False)
```

profile of v0, /device:TPU:1, one launch (start us, length us, event | category | flops | bytes accessed | tf_op | source)
XLA Modules:
  0.0 332.0 jit_solution(8603867656916050667)
XLA Ops:
  7.2 0.0 all-gather.2.cloned.1.call-start
  7.2 0.8 compare_bitcast_fusion
  8.0 0.1 broadcast_bitcast_fusion
  8.1 1.9 broadcast_select_fusion
  10.0 0.0 all-gather.2.cloned.1.call-update
  10.0 0.0 all-reduce.3.cloned.1.call-start
  10.1 79.1 %all-gather.2.cloned.1.call-done = bf16[1536,3072]{1,0:T(8,128)(2,1)} async-done(((bf16[96,3072]{1,0:T(8,128)(2,1)}), bf16[1536,3072]{1,0:T(8,128)(2,1)}) %all-gather.2.cloned.1.call-update) | async-done | bytes 9437200 | tf_op jit(solution)/shard_map/all_gather | solution.py:62
  89.2 5.3 %dynamic-slice_select_fusion = bf16[1536,1536]{1,0:T(8,128)(2,1)} fusion(bf16[1536,3072]{1,0:T(8,128)(2,1)} %all-gather.2.cloned.1.call-done, s32[]{:T(128)S(6)} %select_n.53, pred[]{:T(512)S(6)} %eq.27), kind=kLoop, calls=%fused_computation.4 | loop fusion | flops 2359296 | bytes 9437189 | tf_op jit(solution)/shard_map/jit(_where)/select_n | solution.py:13
  94.5 0.0 all-reduce.3.cloned.1.call-update
  94.5 0.0 reduce-scatter.2.cloned.1.call-start
  94.6 72.9 %all-reduce.3.cloned.1.call-done = bf16[1536,1536]{1,0:T(8,128)(2,1)} async-done(((bf16[1536,1536]{1,0:T(8,128)(2,1)}), bf16[1536,1536]{1,0:T(8,128)(2,1)}) %all-reduce.3.cloned.1.call-update) | async-done | bytes 4718608 | tf_op jit(solution)/shard_map/psum | solution.py:13
  167.5 20.3 %convolution_convert_fusion = bf16[1536,3072]{1,0:T(8,128)(2,1)} fusion(bf16[1536,1536]{1,0:T(8,128)(2,1)} %all-reduce.3.cloned.1.call-done, bf16[3072,1536]{1,0:T(8,128)(2,1)} %param.6), kind=kOutput, calls=%fused_computation.1 | convolution fusion | flops 14500233216 | bytes 23592960 | tf_op jit(solution)/shard_map/dot_general | solution.py:67
  187.8 0.0 copy-start.3
  187.8 0.0 reduce-scatter.2.cloned.1.call-update
  187.8 0.0 copy-start
  187.8 0.6 copy-done.3
  188.5 0.1 iota_compare_fusion
  188.6 0.1 fusion.5
  188.8 0.2 fusion.8
  189.0 3.5 %broadcast_in_dim.39 = f32[384,32,128]{2,1,0:T(8,128)} broadcast(f32[]{:T(128)} %constant.65.clone.1), dimensions={} | broadcast | bytes 6291460 | tf_op jit(solution)/shard_map/broadcast_in_dim | solution.py:92
  192.5 0.0 copy-done
  192.5 23.5 %scatter_fusion = f32[384,32,128]{2,1,0:T(8,128)} fusion(f32[384,32,128]{2,1,0:T(8,128)} %broadcast_in_dim.39, s32[192]{0:T(256)S(1)} %bitcast.46, f32[192,32,128]{2,1,0:T(8,128)S(1)} %copy-done), kind=kCustom, calls=%fused_computation | custom fusion | bytes 9437952 | tf_op jit(solution)/shard_map/scatter | solution.py:94
  216.0 5.3 %convert_element_type.54 = bf16[384,32,128]{2,1,0:T(8,128)(2,1)} convert(f32[384,32,128]{2,1,0:T(8,128)} %scatter_fusion) | non-fusion elementwise | flops 1572864 | bytes 9437184 | tf_op jit(solution)/shard_map/convert_element_type | solution.py:98
  221.3 9.8 %all-to-all-start.1 = ((bf16[128,1,1,3,32,128]{5,4,3,2,1,0:T(8,128)(2,1)}), bf16[128,1,1,3,32,128]{5,4,3,2,1,0:T(8,128)(2,1)S(1)}, u32[]{:S(2)}, u32[]{:S(2)}) async-start(bf16[128,1,1,3,32,128]{5,4,3,2,1,0:T(8,128)(2,1)} %bitcast.38), calls=%async_computation.2 | async-start | bytes 6291456 | tf_op jit(solution)/shard_map/all_to_all | solution.py:39
  231.2 74.3 %reduce-scatter.2.cloned.1.call-done = bf16[96,3072]{1,0:T(8,128)(2,1)} async-done(((bf16[1536,3072]{1,0:T(8,128)(2,1)}), bf16[96,3072]{1,0:T(8,128)(2,1)}) %reduce-scatter.2.cloned.1.call-update) | async-done | bytes 589840 | tf_op jit(solution)/shard_map/reduce_scatter | solution.py:66
  305.5 1.2 select_convert_fusion
  306.7 0.0 copy-start.1
  306.7 0.8 copy-done.1
  307.5 3.9 %fusion.2 = bf16[96,768]{1,0:T(8,128)(2,1)S(1)} fusion(bf16[96,3072]{1,0:T(8,128)(2,1)S(1)} %select_convert_fusion, bf16[1536,3072]{1,0:T(8,128)(2,1)} %all-gather.2.cloned.1.call-done, s32[]{:T(128)S(6)} %select_n.56), kind=kOutput, calls=%fused_computation.7 | convolution fusion | flops 453058560 | bytes 5455876 | tf_op jit(solution)/shard_map/dot_general | solution.py:76
  311.5 0.2 reshape.62
  311.7 0.7 copy.18
  312.4 0.0 all-to-all-done.1
  312.4 6.5 %all-to-all-start = ((bf16[8,96,96]{2,1,0:T(8,128)(2,1)}), bf16[8,96,96]{2,1,0:T(8,128)(2,1)S(1)}, u32[]{:S(2)}, u32[]{:S(2)}) async-start(bf16[8,96,96]{2,1,0:T(8,128)(2,1)} %bitcast.34), calls=%async_computation.1 | async-start | bytes 393216 | tf_op jit(solution)/shard_map/all_to_all | solution.py:23
  318.9 0.0 copy-start.2
  318.9 3.8 %bitcast_convert_fusion = f32[384,32,128]{2,1,0:T(8,128)} fusion(bf16[128,1,1,3,32,128]{5,4,3,2,1,0:T(8,128)(2,1)S(1)} %all-to-all-done.1), kind=kLoop, calls=%fused_computation.5 | loop fusion | flops 1572864 | bytes 9437184 | tf_op jit(solution)/shard_map/convert_element_type | solution.py:99
  322.7 2.1 all-to-all-done
  324.8 0.0 copy-done.2
  324.8 0.6 sub.15
  (9 shorter events, 0.1 us)
Async XLA Ops:
  7.2 82.0 %all-gather.2.cloned.1.call-start = ((), (), s32[]{:S(2)}) async-start(), calls=%async_computation.3 | async-start | bytes 10027008 | tf_op jit(solution)/shard_map/all_gather | solution.py:62
  10.0 157.4 %all-reduce.3.cloned.1.call-start = ((), (), s32[]{:S(2)}) async-start(), calls=%async_computation.4 | async-start | bytes 9437184 | tf_op jit(solution)/shard_map/psum | solution.py:13
  94.5 211.0 %reduce-scatter.2.cloned.1.call-start = ((), (), s32[]{:S(2)}) async-start(), calls=%async_computation.5 | async-start | bytes 10027008 | tf_op jit(solution)/shard_map/reduce_scatter | solution.py:66
  187.8 0.7 copy-start.3
  187.8 4.7 %copy-start = (f32[192,32,128]{2,1,0:T(8,128)S(1)}, f32[192,32,128]{2,1,0:T(8,128)}, u32[]{:S(2)}) copy-start(f32[192,32,128]{2,1,0:T(8,128)} %param.10) | copy-start | bytes 9437188
  221.3 91.1 %all-to-all-start.1 = ((bf16[128,1,1,3,32,128]{5,4,3,2,1,0:T(8,128)(2,1)}), bf16[128,1,1,3,32,128]{5,4,3,2,1,0:T(8,128)(2,1)S(1)}, u32[]{:S(2)}, u32[]{:S(2)}) async-start(bf16[128,1,1,3,32,128]{5,4,3,2,1,0:T(8,128)(2,1)} %bitcast.38), calls=%async_computation.2 | async-start | bytes 6291456 | tf_op jit(solution)/shard_map/all_to_all | solution.py:39
  306.7 0.8 copy-start.1
  312.4 12.3 %all-to-all-start = ((bf16[8,96,96]{2,1,0:T(8,128)(2,1)}), bf16[8,96,96]{2,1,0:T(8,128)(2,1)S(1)}, u32[]{:S(2)}, u32[]{:S(2)}) async-start(bf16[8,96,96]{2,1,0:T(8,128)(2,1)} %bitcast.34), calls=%async_computation.1 | async-start | bytes 393216 | tf_op jit(solution)/shard_map/all_to_all | solution.py:23
  318.9 5.9 %copy-start.2 = (f32[96,96]{1,0:T(8,128)S(1)}, f32[96,96]{1,0:T(8,128)}, u32[]{:S(2)}) copy-start(f32[96,96]{1,0:T(8,128)} %param.8) | copy-start | bytes 110596
Sparse Core Ops, SparseCore 0:
  10.7 78.4 all-gather.1
  94.6 72.7 all-reduce.2
  187.9 117.5 reduce-scatter.1
where the time goes:
time: 333 us; the launch traced here: 332 us
  waiting for transfers between devices  228 us (68%)
  local copies, waits for them, and re-layouts  29.5 us (9%)
  matrix products  24.3 us (7%)
  other arithmetic  19.5 us (6%)
  starting transfers between devices  16.4 us (5%)
  between operations  13.9 us (4%)
    all_gather x1, waiting for transfers between devices, local(): gathered = lax.all_gather(masked, 'col', axis=0, tiled=True)  79.1 us
    reduce_scatter x1, waiting for transfers between devices, local(): lax.psum_scatter(lax.dot_general(cross_rows, ainv_anc, (((1,), (1,)), (()...  74.3 us
    psum x1, waiting for transfers between devices, broadcast(): return lax.psum(jnp.where(mine, value, jnp.zeros_like(value)), axis)  72.9 us
    scatter x1, local copies, waits for them, and re-layouts, local(): buffer = jnp.zeros((devices_all * SLOT, piece_rows, piece_cols), jnp.floa...  23.5 us
    dot_general x1, matrix products, local(): lax.dot_general(cross_rows, ainv_anc, (((1,), (1,)), ((), ())), preferred...  20.3 us
    all_to_all x1, starting transfers between devices, joined_exchange(): parts = lax.all_to_all(parts, axis, split_axis=0, concat_axis=0, tiled=True)  9.85 us
  transfers between devices with their start and end apart: 5, of which 4 were waited for; matrix products, arithmetic and copies ran while one was open for 13% of the time, Pallas kernels for 0%

commit v1 on v0

--- a/solution.py
+++ b/solution.py
@@ -59,7 +59,24 @@
         jnp.broadcast_to(keep_blocks[:, :, None], (1, block_count, AB)).reshape(1, local_rows) > 0
     )
     masked = jnp.where(keep_rows, l_panel, jnp.zeros_like(l_panel))
-    gathered = lax.all_gather(masked, "col", axis=0, tiled=True)
+    step_out = lax.axis_size("col")
+    g_now, next_value, outcome_arr = (step_out, lax.axis_index("col"), masked.shape[0])
+    chunks = tuple(((dev, (dev + 1) % g_now) for dev in range(g_now)))
+    gathered = jnp.zeros((*masked.shape[:0], g_now * outcome_arr, *masked.shape[1:]), masked.dtype)
+    gathered = lax.dynamic_update_slice_in_dim(gathered, masked, next_value * outcome_arr, axis=0)
+    base_arr = out_arr = masked
+    ledger = tuple(((dev, (dev - 1) % g_now) for dev in range(g_now)))
+    upper = g_now // 2
+    for dev_i in range(1, upper + 1):
+        base_arr = lax.ppermute(base_arr, "col", chunks)
+        gathered = lax.dynamic_update_slice_in_dim(
+            gathered, base_arr, (next_value - dev_i) % g_now * outcome_arr, axis=0
+        )
+        if dev_i < g_now - upper:
+            out_arr = lax.ppermute(out_arr, "col", ledger)
+            gathered = lax.dynamic_update_slice_in_dim(
+                gathered, out_arr, (next_value + dev_i) % g_now * outcome_arr, axis=0
+            )
     offset = col_index % group_ratio * cross_width
     own_cross = lax.dynamic_slice_in_dim(gathered, offset, cross_width, 1)
     cross_rows = broadcast(own_cross, "row", col_index // group_ratio)

time: 333 us -> 383 us (1.15)
  starting transfers between devices: 16.4 us -> 51.1 us
  local copies, waits for them, and re-layouts: 29.5 us -> 47.3 us
    all_gather x1 -> x0, waiting for transfers between devices: 79.1 us -> none  [local(): gathered = lax.all_gather(masked, 'col', axis=0, tiled=True)]
    ppermute x0 -> x15, waiting for transfers between devices: none -> 72.9 us  [the longest x8 72.9 us: local(): base_arr = lax.ppermute(base_arr, 'col', chunks)]
    ppermute x0 -> x15, starting transfers between devices: none -> 34.5 us  [the longest x7 32.4 us: local(): out_arr = lax.ppermute(out_arr, 'col', ledger)]
    dynamic_update_slice x0 -> x15, local copies, waits for them, and re-layouts: none -> 12.9 us  [the longest x8 6.86 us: local(): lax.dynamic_update_slice_in_dim(gathered, base_arr, (next_value - dev_i)...]
    broadcast_in_dim x0 -> x1, local copies, waits for them, and re-layouts: none -> 4.84 us  [local(): jnp.zeros((*masked.shape[:0], g_now * outcome_arr, *masked.shape[1:]), ma...]
  transfers between devices with their start and end apart: 5 -> 19, of which waited for: 4 -> 11; matrix products, arithmetic and copies ran while one was open for 13% -> 14% of each run, Pallas kernels for 0% -> 0%
where the time goes in v1:
time: 383 us; the launch traced here: 382 us
  waiting for transfers between devices  226 us (59%)
  starting transfers between devices  51.1 us (13%)
  local copies, waits for them, and re-layouts  47.3 us (12%)
  matrix products  24.4 us (6%)
  other arithmetic  18.6 us (5%)
  between operations  14.2 us (4%)
    psum x1, waiting for transfers between devices, broadcast(): return lax.psum(jnp.where(mine, value, jnp.zeros_like(value)), axis)  76.5 us
    reduce_scatter x1, waiting for transfers between devices, local(): lax.psum_scatter(lax.dot_general(cross_rows, ainv_anc, (((1,), (1,)), (()...  74.5 us
    ppermute x8, waiting for transfers between devices, local(): base_arr = lax.ppermute(base_arr, 'col', chunks)  72.9 us
    ppermute x7, starting transfers between devices, local(): out_arr = lax.ppermute(out_arr, 'col', ledger)  32.4 us
    scatter x1, local copies, waits for them, and re-layouts, local(): buffer = jnp.zeros((devices_all * SLOT, piece_rows, piece_cols), jnp.floa...  23.5 us
    dot_general x1, matrix products, local(): lax.dot_general(cross_rows, ainv_anc, (((1,), (1,)), ((), ())), preferred...  20.5 us
    all_to_all x1, starting transfers between devices, joined_exchange(): parts = lax.all_to_all(parts, axis, split_axis=0, concat_axis=0, tiled=True)  9.88 us
  transfers between devices with their start and end apart: 19, of which 11 were waited for; matrix products, arithmetic and copies ran while one was open for 14% of the time, Pallas kernels for 0%

profile of v1, /device:TPU:1, one launch (start us, length us, event | category | flops | bytes accessed | tf_op | source)
XLA Modules:
  0.0 381.6 jit_solution(13570247056892812192)
XLA Ops:
  7.2 0.0 all-reduce.3.cloned.1.call-start
  7.3 0.8 compare_bitcast_fusion
  8.1 0.1 broadcast_bitcast_fusion
  8.2 4.8 %broadcast_in_dim.39 = bf16[1536,3072]{1,0:T(8,128)(2,1)} broadcast(bf16[]{:T(256)} %constant.142.clone.1), dimensions={} | broadcast | bytes 9437186 | tf_op jit(solution)/shard_map/broadcast_in_dim | solution.py:65
  13.0 1.0 constant_dynamic-update-slice_fusion.15
  14.0 2.0 collective-permute-start
  16.0 3.7 collective-permute-start.1
  19.7 13.0 %collective-permute-done = bf16[96,3072]{1,0:T(8,128)(2,1)S(1)} collective-permute-done((bf16[96,3072]{1,0:T(8,128)(2,1)S(1)}, bf16[96,3072]{1,0:T(8,128)(2,1)S(1)}, u32[]{:S(2)}, u32[]{:S(2)}) %collective-permute-start) | collective-permute-done | bytes 589856 | tf_op jit(solution)/shard_map/ppermute | solution.py:71
  32.7 0.0 collective-permute-start.2
  32.7 0.0 collective-permute-done.1
  32.7 4.8 %collective-permute-start.3 = (bf16[96,3072]{1,0:T(8,128)(2,1)S(1)}, bf16[96,3072]{1,0:T(8,128)(2,1)S(1)}, u32[]{:S(2)}, u32[]{:S(2)}) collective-permute-start(bf16[96,3072]{1,0:T(8,128)(2,1)S(1)} %collective-permute-done.1), channel_id=1, source_target_pairs={{0,15},{1,0},{2,1},{3,2},{4,3},{5,4},{6,5},{7,6},{8,7},{9,8},{10,9... | collective-permute-start | bytes 1769480 | tf_op jit(solution)/shard_map/ppermute | solution.py:76
  37.5 0.8 constant_dynamic-update-slice_fusion.14
  38.3 0.9 constant_dynamic-update-slice_fusion.13
  39.2 10.4 %collective-permute-done.2 = bf16[96,3072]{1,0:T(8,128)(2,1)S(1)} collective-permute-done((bf16[96,3072]{1,0:T(8,128)(2,1)S(1)}, bf16[96,3072]{1,0:T(8,128)(2,1)S(1)}, u32[]{:S(2)}, u32[]{:S(2)}) %collective-permute-start.2) | collective-permute-done | bytes 589856 | tf_op jit(solution)/shard_map/ppermute | solution.py:71
  49.6 4.8 %collective-permute-start.5 = (bf16[96,3072]{1,0:T(8,128)(2,1)S(1)}, bf16[96,3072]{1,0:T(8,128)(2,1)S(1)}, u32[]{:S(2)}, u32[]{:S(2)}) collective-permute-start(bf16[96,3072]{1,0:T(8,128)(2,1)S(1)} %collective-permute-done.3), channel_id=1, source_target_pairs={{0,15},{1,0},{2,1},{3,2},{4,3},{5,4},{6,5},{7,6},{8,7},{9,8},{10,9... | collective-permute-start | bytes 1769480 | tf_op jit(solution)/shard_map/ppermute | solution.py:76
  54.4 0.9 constant_dynamic-update-slice_fusion.12
  55.3 0.9 constant_dynamic-update-slice_fusion.11
  56.1 9.5 %collective-permute-done.4 = bf16[96,3072]{1,0:T(8,128)(2,1)S(1)} collective-permute-done((bf16[96,3072]{1,0:T(8,128)(2,1)S(1)}, bf16[96,3072]{1,0:T(8,128)(2,1)S(1)}, u32[]{:S(2)}, u32[]{:S(2)}) %collective-permute-start.4) | collective-permute-done | bytes 589856 | tf_op jit(solution)/shard_map/ppermute | solution.py:71
  65.7 4.8 %collective-permute-start.7 = (bf16[96,3072]{1,0:T(8,128)(2,1)S(1)}, bf16[96,3072]{1,0:T(8,128)(2,1)S(1)}, u32[]{:S(2)}, u32[]{:S(2)}) collective-permute-start(bf16[96,3072]{1,0:T(8,128)(2,1)S(1)} %collective-permute-done.5), channel_id=1, source_target_pairs={{0,15},{1,0},{2,1},{3,2},{4,3},{5,4},{6,5},{7,6},{8,7},{9,8},{10,9... | collective-permute-start | bytes 1769480 | tf_op jit(solution)/shard_map/ppermute | solution.py:76
  70.5 0.8 constant_dynamic-update-slice_fusion.10
  71.3 0.9 constant_dynamic-update-slice_fusion.9
  72.2 8.7 %collective-permute-done.6 = bf16[96,3072]{1,0:T(8,128)(2,1)S(1)} collective-permute-done((bf16[96,3072]{1,0:T(8,128)(2,1)S(1)}, bf16[96,3072]{1,0:T(8,128)(2,1)S(1)}, u32[]{:S(2)}, u32[]{:S(2)}) %collective-permute-start.6) | collective-permute-done | bytes 589856 | tf_op jit(solution)/shard_map/ppermute | solution.py:71
  80.9 4.8 %collective-permute-start.9 = (bf16[96,3072]{1,0:T(8,128)(2,1)S(1)}, bf16[96,3072]{1,0:T(8,128)(2,1)S(1)}, u32[]{:S(2)}, u32[]{:S(2)}) collective-permute-start(bf16[96,3072]{1,0:T(8,128)(2,1)S(1)} %collective-permute-done.7), channel_id=1, source_target_pairs={{0,15},{1,0},{2,1},{3,2},{4,3},{5,4},{6,5},{7,6},{8,7},{9,8},{10,9... | collective-permute-start | bytes 1769480 | tf_op jit(solution)/shard_map/ppermute | solution.py:76
  85.7 0.9 constant_dynamic-update-slice_fusion.8
  86.5 0.9 constant_dynamic-update-slice_fusion.7
  87.4 7.8 %collective-permute-done.8 = bf16[96,3072]{1,0:T(8,128)(2,1)S(1)} collective-permute-done((bf16[96,3072]{1,0:T(8,128)(2,1)S(1)}, bf16[96,3072]{1,0:T(8,128)(2,1)S(1)}, u32[]{:S(2)}, u32[]{:S(2)}) %collective-permute-start.8) | collective-permute-done | bytes 589856 | tf_op jit(solution)/shard_map/ppermute | solution.py:71
  95.3 4.8 %collective-permute-start.11 = (bf16[96,3072]{1,0:T(8,128)(2,1)S(1)}, bf16[96,3072]{1,0:T(8,128)(2,1)S(1)}, u32[]{:S(2)}, u32[]{:S(2)}) collective-permute-start(bf16[96,3072]{1,0:T(8,128)(2,1)S(1)} %collective-permute-done.9), channel_id=1, source_target_pairs={{0,15},{1,0},{2,1},{3,2},{4,3},{5,4},{6,5},{7,6},{8,7},{9,8},{10,9... | collective-permute-start | bytes 1769480 | tf_op jit(solution)/shard_map/ppermute | solution.py:76
  100.0 0.9 constant_dynamic-update-slice_fusion.6
  100.9 0.9 constant_dynamic-update-slice_fusion.5
  101.8 7.0 %collective-permute-done.10 = bf16[96,3072]{1,0:T(8,128)(2,1)S(1)} collective-permute-done((bf16[96,3072]{1,0:T(8,128)(2,1)S(1)}, bf16[96,3072]{1,0:T(8,128)(2,1)S(1)}, u32[]{:S(2)}, u32[]{:S(2)}) %collective-permute-start.10) | collective-permute-done | bytes 589856 | tf_op jit(solution)/shard_map/ppermute | solution.py:71
  108.7 4.8 %collective-permute-start.13 = (bf16[96,3072]{1,0:T(8,128)(2,1)S(1)}, bf16[96,3072]{1,0:T(8,128)(2,1)S(1)}, u32[]{:S(2)}, u32[]{:S(2)}) collective-permute-start(bf16[96,3072]{1,0:T(8,128)(2,1)S(1)} %collective-permute-done.11), channel_id=1, source_target_pairs={{0,15},{1,0},{2,1},{3,2},{4,3},{5,4},{6,5},{7,6},{8,7},{9,8},{10,9... | collective-permute-start | bytes 1769480 | tf_op jit(solution)/shard_map/ppermute | solution.py:76
  113.5 0.9 constant_dynamic-update-slice_fusion.4
  114.4 0.9 constant_dynamic-update-slice_fusion.3
  115.3 6.1 %collective-permute-done.12 = bf16[96,3072]{1,0:T(8,128)(2,1)S(1)} collective-permute-done((bf16[96,3072]{1,0:T(8,128)(2,1)S(1)}, bf16[96,3072]{1,0:T(8,128)(2,1)S(1)}, u32[]{:S(2)}, u32[]{:S(2)}) %collective-permute-start.12) | collective-permute-done | bytes 589856 | tf_op jit(solution)/shard_map/ppermute | solution.py:71
  121.4 0.8 constant_dynamic-update-slice_fusion.2
  122.2 0.9 constant_dynamic-update-slice_fusion.1
  123.1 10.3 %collective-permute-done.14 = bf16[96,3072]{1,0:T(8,128)(2,1)S(1)} collective-permute-done((bf16[96,3072]{1,0:T(8,128)(2,1)S(1)}, bf16[96,3072]{1,0:T(8,128)(2,1)S(1)}, u32[]{:S(2)}, u32[]{:S(2)}) %collective-permute-start.14) | collective-permute-done | bytes 589856 | tf_op jit(solution)/shard_map/ppermute | solution.py:71
  133.4 0.8 constant_dynamic-update-slice_fusion
  134.3 5.3 %dynamic-slice_select_fusion = bf16[1536,1536]{1,0:T(8,128)(2,1)} fusion(bf16[1536,3072]{1,0:T(8,128)(2,1)} %constant_dynamic-update-slice_fusion, s32[]{:T(128)S(6)} %select_n.192, pred[]{:T(512)S(6)} %eq.42), kind=kLoop, calls=%fused_computation.4 | loop fusion | flops 2359296 | bytes 9437189 | tf_op jit(solution)/shard_map/jit(_where)/select_n | solution.py:13
  139.6 0.0 all-reduce.3.cloned.1.call-update
  139.6 0.2 reduce-scatter.2.cloned.1.call-start
  139.9 76.5 %all-reduce.3.cloned.1.call-done = bf16[1536,1536]{1,0:T(8,128)(2,1)} async-done(((bf16[1536,1536]{1,0:T(8,128)(2,1)}), bf16[1536,1536]{1,0:T(8,128)(2,1)}) %all-reduce.3.cloned.1.call-update) | async-done | bytes 4718608 | tf_op jit(solution)/shard_map/psum | solution.py:13
  216.3 20.5 %convolution_convert_fusion = bf16[1536,3072]{1,0:T(8,128)(2,1)} fusion(bf16[1536,1536]{1,0:T(8,128)(2,1)} %all-reduce.3.cloned.1.call-done, bf16[3072,1536]{1,0:T(8,128)(2,1)} %param.6), kind=kOutput, calls=%fused_computation.1 | convolution fusion | flops 14500233216 | bytes 23592960 | tf_op jit(solution)/shard_map/dot_general | solution.py:84
  236.8 0.0 reduce-scatter.2.cloned.1.call-update
  236.8 0.7 copy-done.4
  237.5 0.1 iota_compare_fusion
  237.6 0.1 fusion.5
  237.8 0.2 fusion.8
  238.0 3.5 broadcast_in_dim.43
  241.5 23.5 %scatter_fusion = f32[384,32,128]{2,1,0:T(8,128)} fusion(f32[384,32,128]{2,1,0:T(8,128)} %broadcast_in_dim.43, s32[192]{0:T(256)S(1)} %bitcast.46, f32[192,32,128]{2,1,0:T(8,128)S(1)} %copy-done), kind=kCustom, calls=%fused_computation | custom fusion | bytes 9437952 | tf_op jit(solution)/shard_map/scatter | solution.py:111
  265.0 5.3 %convert_element_type.54 = bf16[384,32,128]{2,1,0:T(8,128)(2,1)} convert(f32[384,32,128]{2,1,0:T(8,128)} %scatter_fusion) | non-fusion elementwise | flops 1572864 | bytes 9437184 | tf_op jit(solution)/shard_map/convert_element_type | solution.py:115
  270.3 9.9 %all-to-all-start.1 = ((bf16[128,1,1,3,32,128]{5,4,3,2,1,0:T(8,128)(2,1)}), bf16[128,1,1,3,32,128]{5,4,3,2,1,0:T(8,128)(2,1)S(1)}, u32[]{:S(2)}, u32[]{:S(2)}) async-start(bf16[128,1,1,3,32,128]{5,4,3,2,1,0:T(8,128)(2,1)} %bitcast.38), calls=%async_computation.2 | async-start | bytes 6291456 | tf_op jit(solution)/shard_map/all_to_all | solution.py:39
  280.2 0.0 copy-start.3
  280.2 74.5 %reduce-scatter.2.cloned.1.call-done = bf16[96,3072]{1,0:T(8,128)(2,1)} async-done(((bf16[1536,3072]{1,0:T(8,128)(2,1)}), bf16[96,3072]{1,0:T(8,128)(2,1)}) %reduce-scatter.2.cloned.1.call-update) | async-done | bytes 589840 | tf_op jit(solution)/shard_map/reduce_scatter | solution.py:83
  354.8 1.2 select_convert_fusion
  356.0 0.0 copy-start.1
  356.0 0.8 copy-done.1
  356.8 3.9 %fusion.2 = bf16[96,768]{1,0:T(8,128)(2,1)S(1)} fusion(bf16[96,3072]{1,0:T(8,128)(2,1)S(1)} %select_convert_fusion, bf16[1536,3072]{1,0:T(8,128)(2,1)} %constant_dynamic-update-slice_fusion, s32[]{:T(128)S(6)} %select_n.195), kind=kOutput, calls=%fused_computation.7 | convolution fusion | flops 453058560 | bytes 5455876 | tf_op jit(solution)/shard_map/dot_general | solution.py:93
  360.8 0.2 reshape.62
  361.0 0.7 copy.18
  361.7 6.5 %all-to-all-start = ((bf16[8,96,96]{2,1,0:T(8,128)(2,1)}), bf16[8,96,96]{2,1,0:T(8,128)(2,1)S(1)}, u32[]{:S(2)}, u32[]{:S(2)}) async-start(bf16[8,96,96]{2,1,0:T(8,128)(2,1)} %bitcast.34), calls=%async_computation.1 | async-start | bytes 393216 | tf_op jit(solution)/shard_map/all_to_all | solution.py:23
  368.2 3.8 bitcast_convert_fusion
  372.0 2.1 all-to-all-done
  374.1 0.6 sub.47
  (28 shorter events, 0.2 us)
Async XLA Ops:
  7.2 5.8 %copy-start.2 = (bf16[96,3072]{1,0:T(8,128)(2,1)S(1)}, bf16[96,3072]{1,0:T(8,128)(2,1)}, u32[]{:S(2)}) copy-start(bf16[96,3072]{1,0:T(8,128)(2,1)} %param.7) | copy-start | bytes 1769476
  7.2 209.2 %all-reduce.3.cloned.1.call-start = ((), (), s32[]{:S(2)}) async-start(), calls=%async_computation.3 | async-start | bytes 9437184 | tf_op jit(solution)/shard_map/psum | solution.py:13
  14.0 18.7 %collective-permute-start = (bf16[96,3072]{1,0:T(8,128)(2,1)S(1)}, bf16[96,3072]{1,0:T(8,128)(2,1)S(1)}, u32[]{:S(2)}, u32[]{:S(2)}) collective-permute-start(bf16[96,3072]{1,0:T(8,128)(2,1)S(1)} %get-tuple-element.4), channel_id=1, source_target_pairs={{0,1},{1,2},{2,3},{3,4},{4,5},{5,6},{6,7},{7,8},{8,9},{9,10},{10,1... | collective-permute-start | bytes 1769480 | tf_op jit(solution)/shard_map/ppermute | solution.py:71
  16.0 16.7 %collective-permute-start.1 = (bf16[96,3072]{1,0:T(8,128)(2,1)S(1)}, bf16[96,3072]{1,0:T(8,128)(2,1)S(1)}, u32[]{:S(2)}, u32[]{:S(2)}) collective-permute-start(bf16[96,3072]{1,0:T(8,128)(2,1)S(1)} %get-tuple-element.4), channel_id=1, source_target_pairs={{0,15},{1,0},{2,1},{3,2},{4,3},{5,4},{6,5},{7,6},{8,7},{9,8},{10,9... | collective-permute-start | bytes 1769480 | tf_op jit(solution)/shard_map/ppermute | solution.py:76
  32.7 16.9 %collective-permute-start.2 = (bf16[96,3072]{1,0:T(8,128)(2,1)S(1)}, bf16[96,3072]{1,0:T(8,128)(2,1)S(1)}, u32[]{:S(2)}, u32[]{:S(2)}) collective-permute-start(bf16[96,3072]{1,0:T(8,128)(2,1)S(1)} %collective-permute-done), channel_id=1, source_target_pairs={{0,1},{1,2},{2,3},{3,4},{4,5},{5,6},{6,7},{7,8},{8,9},{9,10},{10,1... | collective-permute-start | bytes 1769480 | tf_op jit(solution)/shard_map/ppermute | solution.py:71
  32.7 16.9 %collective-permute-start.3 = (bf16[96,3072]{1,0:T(8,128)(2,1)S(1)}, bf16[96,3072]{1,0:T(8,128)(2,1)S(1)}, u32[]{:S(2)}, u32[]{:S(2)}) collective-permute-start(bf16[96,3072]{1,0:T(8,128)(2,1)S(1)} %collective-permute-done.1), channel_id=1, source_target_pairs={{0,15},{1,0},{2,1},{3,2},{4,3},{5,4},{6,5},{7,6},{8,7},{9,8},{10,9... | collective-permute-start | bytes 1769480 | tf_op jit(solution)/shard_map/ppermute | solution.py:76
  49.6 16.1 %collective-permute-start.4 = (bf16[96,3072]{1,0:T(8,128)(2,1)S(1)}, bf16[96,3072]{1,0:T(8,128)(2,1)S(1)}, u32[]{:S(2)}, u32[]{:S(2)}) collective-permute-start(bf16[96,3072]{1,0:T(8,128)(2,1)S(1)} %collective-permute-done.2), channel_id=1, source_target_pairs={{0,1},{1,2},{2,3},{3,4},{4,5},{5,6},{6,7},{7,8},{8,9},{9,10},{10,1... | collective-permute-start | bytes 1769480 | tf_op jit(solution)/shard_map/ppermute | solution.py:71
  49.6 16.1 %collective-permute-start.5 = (bf16[96,3072]{1,0:T(8,128)(2,1)S(1)}, bf16[96,3072]{1,0:T(8,128)(2,1)S(1)}, u32[]{:S(2)}, u32[]{:S(2)}) collective-permute-start(bf16[96,3072]{1,0:T(8,128)(2,1)S(1)} %collective-permute-done.3), channel_id=1, source_target_pairs={{0,15},{1,0},{2,1},{3,2},{4,3},{5,4},{6,5},{7,6},{8,7},{9,8},{10,9... | collective-permute-start | bytes 1769480 | tf_op jit(solution)/shard_map/ppermute | solution.py:76
  65.7 15.2 %collective-permute-start.6 = (bf16[96,3072]{1,0:T(8,128)(2,1)S(1)}, bf16[96,3072]{1,0:T(8,128)(2,1)S(1)}, u32[]{:S(2)}, u32[]{:S(2)}) collective-permute-start(bf16[96,3072]{1,0:T(8,128)(2,1)S(1)} %collective-permute-done.4), channel_id=1, source_target_pairs={{0,1},{1,2},{2,3},{3,4},{4,5},{5,6},{6,7},{7,8},{8,9},{9,10},{10,1... | collective-permute-start | bytes 1769480 | tf_op jit(solution)/shard_map/ppermute | solution.py:71
  65.7 15.2 %collective-permute-start.7 = (bf16[96,3072]{1,0:T(8,128)(2,1)S(1)}, bf16[96,3072]{1,0:T(8,128)(2,1)S(1)}, u32[]{:S(2)}, u32[]{:S(2)}) collective-permute-start(bf16[96,3072]{1,0:T(8,128)(2,1)S(1)} %collective-permute-done.5), channel_id=1, source_target_pairs={{0,15},{1,0},{2,1},{3,2},{4,3},{5,4},{6,5},{7,6},{8,7},{9,8},{10,9... | collective-permute-start | bytes 1769480 | tf_op jit(solution)/shard_map/ppermute | solution.py:76
  80.9 14.4 %collective-permute-start.8 = (bf16[96,3072]{1,0:T(8,128)(2,1)S(1)}, bf16[96,3072]{1,0:T(8,128)(2,1)S(1)}, u32[]{:S(2)}, u32[]{:S(2)}) collective-permute-start(bf16[96,3072]{1,0:T(8,128)(2,1)S(1)} %collective-permute-done.6), channel_id=1, source_target_pairs={{0,1},{1,2},{2,3},{3,4},{4,5},{5,6},{6,7},{7,8},{8,9},{9,10},{10,1... | collective-permute-start | bytes 1769480 | tf_op jit(solution)/shard_map/ppermute | solution.py:71
  80.9 14.4 %collective-permute-start.9 = (bf16[96,3072]{1,0:T(8,128)(2,1)S(1)}, bf16[96,3072]{1,0:T(8,128)(2,1)S(1)}, u32[]{:S(2)}, u32[]{:S(2)}) collective-permute-start(bf16[96,3072]{1,0:T(8,128)(2,1)S(1)} %collective-permute-done.7), channel_id=1, source_target_pairs={{0,15},{1,0},{2,1},{3,2},{4,3},{5,4},{6,5},{7,6},{8,7},{9,8},{10,9... | collective-permute-start | bytes 1769480 | tf_op jit(solution)/shard_map/ppermute | solution.py:76
  95.2 13.5 %collective-permute-start.10 = (bf16[96,3072]{1,0:T(8,128)(2,1)S(1)}, bf16[96,3072]{1,0:T(8,128)(2,1)S(1)}, u32[]{:S(2)}, u32[]{:S(2)}) collective-permute-start(bf16[96,3072]{1,0:T(8,128)(2,1)S(1)} %collective-permute-done.8), channel_id=1, source_target_pairs={{0,1},{1,2},{2,3},{3,4},{4,5},{5,6},{6,7},{7,8},{8,9},{9,10},{10,1... | collective-permute-start | bytes 1769480 | tf_op jit(solution)/shard_map/ppermute | solution.py:71
  95.3 13.5 %collective-permute-start.11 = (bf16[96,3072]{1,0:T(8,128)(2,1)S(1)}, bf16[96,3072]{1,0:T(8,128)(2,1)S(1)}, u32[]{:S(2)}, u32[]{:S(2)}) collective-permute-start(bf16[96,3072]{1,0:T(8,128)(2,1)S(1)} %collective-permute-done.9), channel_id=1, source_target_pairs={{0,15},{1,0},{2,1},{3,2},{4,3},{5,4},{6,5},{7,6},{8,7},{9,8},{10,9... | collective-permute-start | bytes 1769480 | tf_op jit(solution)/shard_map/ppermute | solution.py:76
  108.7 12.6 %collective-permute-start.12 = (bf16[96,3072]{1,0:T(8,128)(2,1)S(1)}, bf16[96,3072]{1,0:T(8,128)(2,1)S(1)}, u32[]{:S(2)}, u32[]{:S(2)}) collective-permute-start(bf16[96,3072]{1,0:T(8,128)(2,1)S(1)} %collective-permute-done.10), channel_id=1, source_target_pairs={{0,1},{1,2},{2,3},{3,4},{4,5},{5,6},{6,7},{7,8},{8,9},{9,10},{10,1... | collective-permute-start | bytes 1769480 | tf_op jit(solution)/shard_map/ppermute | solution.py:71
  108.7 13.5 %collective-permute-start.13 = (bf16[96,3072]{1,0:T(8,128)(2,1)S(1)}, bf16[96,3072]{1,0:T(8,128)(2,1)S(1)}, u32[]{:S(2)}, u32[]{:S(2)}) collective-permute-start(bf16[96,3072]{1,0:T(8,128)(2,1)S(1)} %collective-permute-done.11), channel_id=1, source_target_pairs={{0,15},{1,0},{2,1},{3,2},{4,3},{5,4},{6,5},{7,6},{8,7},{9,8},{10,9... | collective-permute-start | bytes 1769480 | tf_op jit(solution)/shard_map/ppermute | solution.py:76
  121.4 12.1 %collective-permute-start.14 = (bf16[96,3072]{1,0:T(8,128)(2,1)S(1)}, bf16[96,3072]{1,0:T(8,128)(2,1)S(1)}, u32[]{:S(2)}, u32[]{:S(2)}) collective-permute-start(bf16[96,3072]{1,0:T(8,128)(2,1)S(1)} %collective-permute-done.12), channel_id=1, source_target_pairs={{0,1},{1,2},{2,3},{3,4},{4,5},{5,6},{6,7},{7,8},{8,9},{9,10},{10,1... | collective-permute-start | bytes 1769480 | tf_op jit(solution)/shard_map/ppermute | solution.py:71
  139.6 215.1 %reduce-scatter.2.cloned.1.call-start = ((), (), s32[]{:S(2)}) async-start(), calls=%async_computation.4 | async-start | bytes 10027008 | tf_op jit(solution)/shard_map/reduce_scatter | solution.py:83
  236.8 0.7 copy-start.4
  236.8 4.7 %copy-start = (f32[192,32,128]{2,1,0:T(8,128)S(1)}, f32[192,32,128]{2,1,0:T(8,128)}, u32[]{:S(2)}) copy-start(f32[192,32,128]{2,1,0:T(8,128)} %param.10) | copy-start | bytes 9437188
  270.3 91.4 %all-to-all-start.1 = ((bf16[128,1,1,3,32,128]{5,4,3,2,1,0:T(8,128)(2,1)}), bf16[128,1,1,3,32,128]{5,4,3,2,1,0:T(8,128)(2,1)S(1)}, u32[]{:S(2)}, u32[]{:S(2)}) async-start(bf16[128,1,1,3,32,128]{5,4,3,2,1,0:T(8,128)(2,1)} %bitcast.38), calls=%async_computation.2 | async-start | bytes 6291456 | tf_op jit(solution)/shard_map/all_to_all | solution.py:39
  280.2 93.9 %copy-start.3 = (f32[96,96]{1,0:T(8,128)S(1)}, f32[96,96]{1,0:T(8,128)}, u32[]{:S(2)}) copy-start(f32[96,96]{1,0:T(8,128)} %param.8) | copy-start | bytes 110596
  356.0 0.8 copy-start.1
  361.7 12.3 %all-to-all-start = ((bf16[8,96,96]{2,1,0:T(8,128)(2,1)}), bf16[8,96,96]{2,1,0:T(8,128)(2,1)S(1)}, u32[]{:S(2)}, u32[]{:S(2)}) async-start(bf16[8,96,96]{2,1,0:T(8,128)(2,1)} %bitcast.34), calls=%async_computation.1 | async-start | bytes 393216 | tf_op jit(solution)/shard_map/all_to_all | solution.py:23
Sparse Core Ops, SparseCore 0:
  139.8 76.5 all-reduce.2
  236.9 117.7 reduce-scatter.1
